TPU v7x, 32 devices: a whole 2x2x4 slice. The times are simulated.
32 devices in a mesh: eq: 2 (over x), row: 4 (over y, core), col: 4 (over z).
Axes of the slice: x: 2, y: 2, z: 4, core: 2. Of those that a mesh axis runs over, the one named last changes fastest.
Arguments:
- transition: float32 [6144, 3072], P(('eq', 'row'), 'col'), parts along dimension 0, may hold values from -0.05 to 0.9
- covariance: float32 [6144, 3072], P(('eq', 'row'), 'col'), parts along dimension 0, may hold values from -1 to 5, as said below
Outputs:
- covariance_out: float32 [6144, 3072], P(('eq', 'row'), 'col'), parts along dimension 0
- transition_out: float32 [6144, 3072], P(('eq', 'row'), 'col'), parts along dimension 0
There are 2 independent parts, one for each index of `eq`. A program takes and returns all parts, laid end to end along the dimension named above; each array names one. Nothing has to cross between parts.
Inputs may be any that keep to these rules, and one draw needn't show every extreme that they name: covariance is exactly symmetric.
All inputs are finite; a program needn't handle non-finite values.
Results may differ from a plain program's by a relative error of at most 0.0001.
Values sent between devices are 32-bit elements; how exact they have to be, the bound alone decides.
No kernel may reach another device: no remote copies, remote signals or barrier semaphores. Data moves between devices by JAX's collectives and lax.ppermute only.
A program may use at most 128 MiB of HBM per device.

v0:
```python
import jax
import jax.numpy as jnp
from jax import lax
from jax.sharding import PartitionSpec as P


def per_device(transition, covariance):
    highest = lax.Precision.HIGHEST
    current = covariance
    matrix_row = lax.all_gather(transition, "col", axis=1, tiled=True)

    def add_one(pieces):
        return jnp.dot(matrix_row, pieces, precision=highest, preferred_element_type=jnp.float32)

    row_slices = lax.all_to_all(
        lax.all_to_all(transition, "row", split_axis=0, concat_axis=1, tiled=True),
        "col",
        split_axis=1,
        concat_axis=1,
        tiled=True,
    )
    product = add_one(lax.all_gather(current, "row", axis=0, tiled=True))
    squared = add_one(lax.all_gather(transition, "row", axis=0, tiled=True))
    product_row = lax.all_gather(product, "col", axis=1, tiled=True)
    update = lax.dot_general(
        product_row,
        lax.all_gather(row_slices, "row", axis=0, tiled=True),
        (((1,), (1,)), ((), ())),
        precision=highest,
        preferred_element_type=jnp.float32,
    )
    current = update + current
    return (current, squared)


def solution(mesh):
    return jax.shard_map(
        per_device,
        mesh=mesh,
        in_specs=(P(("eq", "row"), "col"), P(("eq", "row"), "col")),
        out_specs=(P(("eq", "row"), "col"), P(("eq", "row"), "col")),
        check_vma=False,
    )
```

profile of v0, /device:TPU:0, one launch (start us, length us, event | category | flops | bytes accessed | tf_op | source)
XLA Modules:
  0.0 605.5 jit_solution(9923091636029613894)
XLA Ops:
  7.2 0.0 all-gather.8.cloned.1.call-start
  7.2 0.7 all-gather.8.cloned.1.call-update
  7.9 0.0 all-gather.6.cloned.1.call-start
  7.9 0.7 all-gather.6.cloned.1.call-update
  8.6 0.0 all-gather.14.cloned.1.call-start
  8.7 0.7 all-gather.14.cloned.1.call-update
  9.4 0.0 all-gather.12.cloned.1.call-start
  9.4 51.7 %all_to_all.25 = f32[4,192,768]{2,1,0:T(8,128)S(1)} all-to-all(f32[4,192,768]{2,1,0:T(8,128)} %bitcast.10), channel_id=1, replica_groups=mesh['eq'=2,'row'=4,'col'=4] {'row'}, dimensions={0} | all-to-all | bytes 4718592 | tf_op jit(solution)/shard_map/all_to_all | solution.py:16
  61.1 88.7 %all_to_all.26 = f32[192,4,768]{2,0,1:T(8,128)S(1)} all-to-all(f32[192,4,768]{2,0,1:T(8,128)S(1)} %bitcast.13), channel_id=1, replica_groups=mesh['eq'=2,'row'=4,'col'=4] {'col'}, dimensions={1} | all-to-all | bytes 4718592 | tf_op jit(solution)/shard_map/all_to_all | solution.py:15
  149.8 1.6 copy.6
  151.5 0.0 all-gather.12.cloned.1.call-update
  151.5 0.0 all-gather.10.cloned.1.call-start
  151.5 0.0 all-gather.8.cloned.1.call-done
  151.6 121.3 %all-gather.6.cloned.1.call-done = f32[768,3072]{1,0:T(8,128)} async-done(((f32[768,768]{1,0:T(8,128)}), f32[768,3072]{1,0:T(8,128)}) %all-gather.6.cloned.1.call-update) | async-done | bytes 9437200 | tf_op jit(solution)/shard_map/all_gather | solution.py:10
  272.8 27.4 %fusion = f32[768,768]{1,0:T(8,128)} fusion(f32[768,3072]{1,0:T(8,128)} %all-gather.6.cloned.1.call-done, f32[3072,768]{1,0:T(8,128)} %all-gather.8.cloned.1.call-done), kind=kOutput, calls=%fused_computation.1 | convolution fusion | flops 21743271936 | bytes 21233664 | tf_op jit(solution)/shard_map/dot_general | solution.py:13
  300.2 0.0 all-gather.10.cloned.1.call-update
  300.3 0.0 copy-start
  300.3 36.6 %all-gather.14.cloned.1.call-done = f32[3072,768]{1,0:T(8,128)} async-done(((f32[768,768]{1,0:T(8,128)}), f32[3072,768]{1,0:T(8,128)}) %all-gather.14.cloned.1.call-update) | async-done | bytes 9437200 | tf_op jit(solution)/shard_map/all_gather | solution.py:23
  336.9 27.4 %fusion.1 = f32[768,768]{1,0:T(8,128)} fusion(f32[768,3072]{1,0:T(8,128)} %all-gather.6.cloned.1.call-done, f32[3072,768]{1,0:T(8,128)} %all-gather.14.cloned.1.call-done), kind=kOutput, calls=%fused_computation.2 | convolution fusion | flops 21743271936 | bytes 21233664 | tf_op jit(solution)/shard_map/dot_general | solution.py:13
  364.3 38.3 %all-gather.12.cloned.1.call-done = f32[768,3072]{1,0:T(8,128)} async-done(((f32[192,3072]{1,0:T(8,128)}), f32[768,3072]{1,0:T(8,128)}) %all-gather.12.cloned.1.call-update) | async-done | bytes 9437200 | tf_op jit(solution)/shard_map/all_gather | solution.py:27
  402.5 168.8 %all-gather.10.cloned.1.call-done = f32[768,3072]{1,0:T(8,128)} async-done(((f32[768,768]{1,0:T(8,128)}), f32[768,3072]{1,0:T(8,128)}) %all-gather.10.cloned.1.call-update) | async-done | bytes 9437200 | tf_op jit(solution)/shard_map/all_gather | solution.py:24
  571.3 0.0 copy-done
  571.3 27.7 %convolution_add_fusion = f32[768,768]{1,0:T(8,128)} fusion(f32[768,768]{1,0:T(8,128)S(1)} %copy-done, f32[768,3072]{1,0:T(8,128)} %all-gather.10.cloned.1.call-done, f32[768,3072]{1,0:T(8,128)} %all-gather.12.cloned.1.call-done), kind=kOutput, calls=%fused_computation | convolution fusion | flops 21743861760 | bytes 23592960 | tf_op jit(solution)/shard_map/dot_general | solution.py:25
Async XLA Ops:
  7.2 144.4 %all-gather.8.cloned.1.call-start = ((), (), s32[]{:S(2)}) async-start(), calls=%async_computation.3 | async-start | bytes 11796480 | tf_op jit(solution)/shard_map/all_gather | solution.py:22
  7.9 264.9 %all-gather.6.cloned.1.call-start = ((), (), s32[]{:S(2)}) async-start(), calls=%async_computation.2 | async-start | bytes 11796480 | tf_op jit(solution)/shard_map/all_gather | solution.py:10
  8.6 328.2 %all-gather.14.cloned.1.call-start = ((), (), s32[]{:S(2)}) async-start(), calls=%async_computation.6 | async-start | bytes 11796480 | tf_op jit(solution)/shard_map/all_gather | solution.py:23
  9.4 393.2 %all-gather.12.cloned.1.call-start = ((), (), s32[]{:S(2)}) async-start(), calls=%async_computation.5 | async-start | bytes 11796480 | tf_op jit(solution)/shard_map/all_gather | solution.py:27
  151.5 419.8 %all-gather.10.cloned.1.call-start = ((), (), s32[]{:S(2)}) async-start(), calls=%async_computation.4 | async-start | bytes 11796480 | tf_op jit(solution)/shard_map/all_gather | solution.py:24
  300.3 271.0 %copy-start = (f32[768,768]{1,0:T(8,128)S(1)}, f32[768,768]{1,0:T(8,128)}, u32[]{:S(2)}) copy-start(f32[768,768]{1,0:T(8,128)} %param.3) | copy-start | bytes 7077892
Sparse Core Ops, SparseCore 0:
  9.5 85.0 all-gather.7
  96.2 176.6 all-gather.5
  274.4 62.4 all-gather.13
  338.3 64.2 all-gather.11
  404.5 166.7 all-gather.9
where the time goes:
time: 606 us
  waiting for transfers between devices  367 us (61%)
  blocking collectives  140 us (23%)
  matrix products  82.5 us (14%)
  between operations  13.8 us (2%)
    all_gather x1, waiting for transfers between devices, per_device(): product_row = lax.all_gather(product, 'col', axis=1, tiled=True)  169 us
    all_gather x1, waiting for transfers between devices, per_device(): matrix_row = lax.all_gather(transition, 'col', axis=1, tiled=True)  121 us
    all_to_all x1, blocking collectives, per_device(): lax.all_to_all(lax.all_to_all(transition, 'row', split_axis=0, concat_axi...  88.7 us
    dot_general x2, matrix products, add_one(): jnp.dot(matrix_row, pieces, precision=highest, preferred_element_type=jnp...  54.8 us
    all_to_all x1, blocking collectives, per_device(): lax.all_to_all(transition, 'row', split_axis=0, concat_axis=1, tiled=True)  51.7 us
    all_gather x1, waiting for transfers between devices, per_device(): lax.all_gather(row_slices, 'row', axis=0, tiled=True)  38.3 us
    all_gather x1, waiting for transfers between devices, per_device(): squared = add_one(lax.all_gather(transition, 'row', axis=0, tiled=True))  36.6 us
    dot_general x1, matrix products, per_device(): lax.dot_general(product_row, lax.all_gather(row_slices, 'row', axis=0, ti...  27.7 us
  transfers between devices with their start and end apart: 5, of which 4 were waited for; matrix products, arithmetic and copies ran while one was open for 9% of the time, Pallas kernels for 0%

commit v1 on v0

--- a/solution.py
+++ b/solution.py
@@ -7,7 +7,12 @@
 def per_device(transition, covariance):
     highest = lax.Precision.HIGHEST
     current = covariance
-    matrix_row = lax.all_gather(transition, "col", axis=1, tiled=True)
+    ring = [transition]
+    for hop in range(3):
+        ring.append(lax.ppermute(ring[-1], "col", [(dev, (dev + 1) % 4) for dev in range(4)]))
+    matrix_row = jnp.roll(
+        jnp.concatenate(ring[::-1], axis=1), (lax.axis_index("col") + 1) * ring[0].shape[1], axis=1
+    )
 
     def add_one(pieces):
         return jnp.dot(matrix_row, pieces, precision=highest, preferred_element_type=jnp.float32)

time: 606 us -> 527 us (0.87)
  waiting for transfers between devices: 367 us -> 296 us
  blocking collectives: 140 us -> 110 us
  local copies, waits for them, and re-layouts: 1.64 us -> 22.8 us
    ppermute x0 -> x3, waiting for transfers between devices: none -> 158 us  [per_device(): lax.ppermute(ring[-1], 'col', [(dev, (dev + 1) % 4) for dev in range(4)])]
    all_gather x1 -> x0, waiting for transfers between devices: 121 us -> none  [per_device(): matrix_row = lax.all_gather(transition, 'col', axis=1, tiled=True)]
    all_gather x1, waiting for transfers between devices: 38.3 us -> 0.01 us  [per_device(): lax.all_gather(row_slices, 'row', axis=0, tiled=True)]
    all_gather x1, waiting for transfers between devices: 36.6 us -> 0.02 us  [per_device(): squared = add_one(lax.all_gather(transition, 'row', axis=0, tiled=True))]
    all_gather x1, waiting for transfers between devices: 169 us -> 136 us  [per_device(): product_row = lax.all_gather(product, 'col', axis=1, tiled=True)]
    all_to_all x1, blocking collectives: 88.7 us -> 59.3 us  [per_device(): lax.all_to_all(lax.all_to_all(transition, 'row', split_axis=0, concat_axi...]
    unnamed x2 -> x15, local copies, waits for them, and re-layouts: 0.01 us -> 19.5 us
  transfers between devices with their start and end apart: 5 -> 7, of which waited for: 4 -> 4; matrix products, arithmetic and copies ran while one was open for 9% -> 15% of each run, Pallas kernels for 0% -> 0%
where the time goes in v1:
time: 527 us
  waiting for transfers between devices  296 us (56%)
  blocking collectives  110 us (21%)
  matrix products  83.2 us (16%)
  local copies, waits for them, and re-layouts  22.8 us (4%)
  between operations  13.8 us (3%)
    ppermute x3, waiting for transfers between devices, per_device(): lax.ppermute(ring[-1], 'col', [(dev, (dev + 1) % 4) for dev in range(4)])  158 us
    all_gather x1, waiting for transfers between devices, per_device(): product_row = lax.all_gather(product, 'col', axis=1, tiled=True)  136 us
    all_to_all x1, blocking collectives, per_device(): lax.all_to_all(lax.all_to_all(transition, 'row', split_axis=0, concat_axi...  59.3 us
    dot_general x2, matrix products, add_one(): jnp.dot(matrix_row, pieces, precision=highest, preferred_element_type=jnp...  55.5 us
    all_to_all x1, blocking collectives, per_device(): lax.all_to_all(transition, 'row', split_axis=0, concat_axis=1, tiled=True)  51 us
    dot_general x1, matrix products, per_device(): lax.dot_general(product_row, lax.all_gather(row_slices, 'row', axis=0, ti...  27.7 us
    unnamed x15, local copies, waits for them, and re-layouts  19.5 us
  transfers between devices with their start and end apart: 7, of which 4 were waited for; matrix products, arithmetic and copies ran while one was open for 15% of the time, Pallas kernels for 0%

profile of v1, /device:TPU:0, one launch (start us, length us, event | category | flops | bytes accessed | tf_op | source)
XLA Modules:
  0.0 526.7 jit_solution(3963260875512785808)
XLA Ops:
  7.2 0.0 all-gather.5.cloned.1.call-start
  7.2 0.7 all-gather.5.cloned.1.call-update
  7.9 0.0 copy-start
  7.9 0.0 all-gather.11.cloned.1.call-start
  8.0 0.7 all-gather.11.cloned.1.call-update
  8.7 0.0 all-gather.9.cloned.1.call-start
  8.7 51.0 %all_to_all.25 = f32[4,192,768]{2,1,0:T(8,128)S(1)} all-to-all(f32[4,192,768]{2,1,0:T(8,128)} %bitcast.8), channel_id=1, replica_groups=mesh['eq'=2,'row'=4,'col'=4] {'row'}, dimensions={0} | all-to-all | bytes 4718592 | tf_op jit(solution)/shard_map/all_to_all | solution.py:21
  59.7 59.3 %all_to_all.26 = f32[192,4,768]{2,0,1:T(8,128)S(1)} all-to-all(f32[192,4,768]{2,0,1:T(8,128)S(1)} %bitcast.11), channel_id=1, replica_groups=mesh['eq'=2,'row'=4,'col'=4] {'col'}, dimensions={1} | all-to-all | bytes 4718592 | tf_op jit(solution)/shard_map/all_to_all | solution.py:20
  119.0 1.6 copy.6
  120.7 0.0 all-gather.9.cloned.1.call-update
  120.7 0.0 all-gather.7.cloned.1.call-start
  120.7 0.0 copy-done
  120.8 0.3 collective-permute-start
  121.0 53.4 %collective-permute-done = f32[768,768]{1,0:T(8,128)S(1)} collective-permute-done((f32[768,768]{1,0:T(8,128)S(1)}, f32[768,768]{1,0:T(8,128)S(1)}, u32[]{:S(2)}, u32[]{:S(2)}) %collective-permute-start) | collective-permute-done | bytes 2359328 | tf_op jit(solution)/shard_map/ppermute | solution.py:12
  174.4 0.0 copy-start.1
  174.4 1.4 copy-done.1
  175.8 0.0 collective-permute-start.1
  175.8 52.8 %collective-permute-done.1 = f32[768,768]{1,0:T(8,128)} collective-permute-done((f32[768,768]{1,0:T(8,128)S(1)}, f32[768,768]{1,0:T(8,128)}, u32[]{:S(2)}, u32[]{:S(2)}) %collective-permute-start.1) | collective-permute-done | bytes 2359328 | tf_op jit(solution)/shard_map/ppermute | solution.py:12
  228.6 0.0 collective-permute-start.2
  228.6 0.0 copy-start.2
  228.6 52.2 %collective-permute-done.2 = f32[768,768]{1,0:T(8,128)} collective-permute-done((f32[768,768]{1,0:T(8,128)}, f32[768,768]{1,0:T(8,128)}, u32[]{:S(2)}, u32[]{:S(2)}) %collective-permute-start.2) | collective-permute-done | bytes 2359328 | tf_op jit(solution)/shard_map/ppermute | solution.py:12
  280.8 3.3 constant_dynamic-update-slice_fusion.7
  284.1 3.3 constant_dynamic-update-slice_fusion.6
  287.5 0.0 copy-done.2
  287.5 1.6 constant_dynamic-update-slice_fusion.5
  289.0 1.6 constant_dynamic-update-slice_fusion.4
  290.7 3.4 constant_dynamic-update-slice_fusion.3
  294.0 3.3 constant_dynamic-update-slice_fusion.2
  297.3 1.6 constant_dynamic-update-slice_fusion.1
  298.9 1.7 constant_dynamic-update-slice_fusion
  300.6 0.0 all-gather.5.cloned.1.call-done
  300.6 27.7 %fusion.2 = f32[768,768]{1,0:T(8,128)} fusion(f32[3072,768]{1,0:T(8,128)} %all-gather.5.cloned.1.call-done, f32[768,6144]{1,0:T(8,128)} %constant_dynamic-update-slice_fusion, s32[]{:T(128)S(6)} %select_n.14), kind=kOutput, calls=%fused_computation.2 | convolution fusion | flops 21743271936 | bytes 21233668 | tf_op jit(solution)/shard_map/dot_general | solution.py:18
  328.3 0.0 all-gather.7.cloned.1.call-update
  328.3 0.0 copy-start.3
  328.3 0.0 all-gather.11.cloned.1.call-done
  328.3 27.8 %fusion = f32[768,768]{1,0:T(8,128)} fusion(f32[3072,768]{1,0:T(8,128)} %all-gather.11.cloned.1.call-done, f32[768,6144]{1,0:T(8,128)} %constant_dynamic-update-slice_fusion, s32[]{:T(128)S(6)} %select_n.14), kind=kOutput, calls=%fused_computation | convolution fusion | flops 21743271936 | bytes 21233668 | tf_op jit(solution)/shard_map/dot_general | solution.py:18
  356.2 0.0 all-gather.9.cloned.1.call-done
  356.2 136.3 %all-gather.7.cloned.1.call-done = f32[768,3072]{1,0:T(8,128)} async-done(((f32[768,768]{1,0:T(8,128)}), f32[768,3072]{1,0:T(8,128)}) %all-gather.7.cloned.1.call-update) | async-done | bytes 9437200 | tf_op jit(solution)/shard_map/all_gather | solution.py:29
  492.5 0.0 copy-done.3
  492.5 27.7 %convolution_add_fusion = f32[768,768]{1,0:T(8,128)} fusion(f32[768,768]{1,0:T(8,128)S(1)} %copy-done.3, f32[768,3072]{1,0:T(8,128)} %all-gather.7.cloned.1.call-done, f32[768,3072]{1,0:T(8,128)} %all-gather.9.cloned.1.call-done), kind=kOutput, calls=%fused_computation.4 | convolution fusion | flops 21743861760 | bytes 23592960 | tf_op jit(solution)/shard_map/dot_general | solution.py:30
Async XLA Ops:
  7.2 293.4 %all-gather.5.cloned.1.call-start = ((), (), s32[]{:S(2)}) async-start(), calls=%async_computation.2 | async-start | bytes 11796480 | tf_op jit(solution)/shard_map/all_gather | solution.py:27
  7.9 112.9 %copy-start = (f32[768,768]{1,0:T(8,128)S(1)}, f32[768,768]{1,0:T(8,128)}, u32[]{:S(2)}) copy-start(f32[768,768]{1,0:T(8,128)} %param.2) | copy-start | bytes 7077892
  7.9 320.4 %all-gather.11.cloned.1.call-start = ((), (), s32[]{:S(2)}) async-start(), calls=%async_computation.5 | async-start | bytes 11796480 | tf_op jit(solution)/shard_map/all_gather | solution.py:28
  8.7 347.5 %all-gather.9.cloned.1.call-start = ((), (), s32[]{:S(2)}) async-start(), calls=%async_computation.4 | async-start | bytes 11796480 | tf_op jit(solution)/shard_map/all_gather | solution.py:32
  120.7 371.8 %all-gather.7.cloned.1.call-start = ((), (), s32[]{:S(2)}) async-start(), calls=%async_computation.3 | async-start | bytes 11796480 | tf_op jit(solution)/shard_map/all_gather | solution.py:29
  120.8 53.6 %collective-permute-start = (f32[768,768]{1,0:T(8,128)S(1)}, f32[768,768]{1,0:T(8,128)S(1)}, u32[]{:S(2)}, u32[]{:S(2)}) collective-permute-start(f32[768,768]{1,0:T(8,128)S(1)} %copy-done), channel_id=1, source_target_pairs={{0,1},{1,2},{2,3},{3,0},{4,5},{5,6},{6,7},{7,4},{8,9},{9,10},{10,1... | collective-permute-start | bytes 7077896 | tf_op jit(solution)/shard_map/ppermute | solution.py:12
  174.4 1.4 copy-start.1
  175.8 52.8 %collective-permute-start.1 = (f32[768,768]{1,0:T(8,128)S(1)}, f32[768,768]{1,0:T(8,128)}, u32[]{:S(2)}, u32[]{:S(2)}) collective-permute-start(f32[768,768]{1,0:T(8,128)S(1)} %collective-permute-done), channel_id=1, source_target_pairs={{0,1},{1,2},{2,3},{3,0},{4,5},{5,6},{6,7},{7,4},{8,9},{9,10},{10,1... | collective-permute-start | bytes 7077896 | tf_op jit(solution)/shard_map/ppermute | solution.py:12
  228.6 52.2 %collective-permute-start.2 = (f32[768,768]{1,0:T(8,128)}, f32[768,768]{1,0:T(8,128)}, u32[]{:S(2)}, u32[]{:S(2)}) collective-permute-start(f32[768,768]{1,0:T(8,128)} %collective-permute-done.1), channel_id=1, source_target_pairs={{0,1},{1,2},{2,3},{3,0},{4,5},{5,6},{6,7},{7,4},{8,9},{9,10},{10,1... | collective-permute-start | bytes 7077896 | tf_op jit(solution)/shard_map/ppermute | solution.py:12
  228.6 58.8 %copy-start.2 = (f32[768,768]{1,0:T(8,128)S(1)}, f32[768,768]{1,0:T(8,128)}, u32[]{:S(2)}) copy-start(f32[768,768]{1,0:T(8,128)} %copy-done.1) | copy-start | bytes 7077892
  328.3 164.2 %copy-start.3 = (f32[768,768]{1,0:T(8,128)S(1)}, f32[768,768]{1,0:T(8,128)}, u32[]{:S(2)}) copy-start(f32[768,768]{1,0:T(8,128)} %param.3) | copy-start | bytes 7077892
Sparse Core Ops, SparseCore 0:
  9.5 84.3 all-gather.4
  95.4 65.2 all-gather.10
  162.3 64.2 all-gather.8
  328.4 164.0 all-gather.6
